TPU v7x, 32 devices: a whole 2x2x4 slice. The times are simulated.
32 devices in a mesh: grp: 4 (over x, core), clu: 8 (over z, y).
Axes of the slice: x: 2, y: 2, z: 4, core: 2. Of those that a mesh axis runs over, the one named last changes fastest.
Arguments:
- radiosity: float32 [128, 3, 128], P(('grp', 'clu')), may hold values from 0 to 3
- form_factors: float32 [4096, 128, 128], P(('grp', 'clu')), may hold values from 0.01 to 16
- source_device: int32 [4096, 1], P(('grp', 'clu')), may hold values from 0 to 31; in each aligned block of 128 rows (0 to 127, 128 to 255, ...) at most 8 rows name the same one
- source_slot: int32 [4096], P(('grp', 'clu')), may hold values from 0 to 3
- receiver_slot: int32 [4096], P(('grp', 'clu')), may hold values from 0 to 3
- emission: float32 [128, 3, 128], P(('grp', 'clu')), may hold values from 0.1 to 2
- reflectance: float32 [128, 3, 128], P(('grp', 'clu')), may hold values from 0.3 to 0.9
- patch_area: float32 [128, 128], P(('grp', 'clu')), may hold values from 0.5 to 2
- cluster_group: int32 [128], P(('grp', 'clu')), may hold values from 0 to 15, as said below
- group_coupling: float32 [16, 16], replicated, may hold values from 0 to 1
- ambient: float32 [3], replicated, may hold values from 0.2 to 1
Outputs:
- radiosity_new: float32 [128, 3, 128], P(('grp', 'clu'))
- group_radiosity: float32 [16, 3], replicated
Inputs may be any that keep to these rules, and one draw needn't show every extreme that they name: `source_device`: the rows of one device name each source device at most 8 times. `cluster_group`: each group node has exactly 8 clusters.
All inputs are finite; a program needn't handle non-finite values.
Results may differ from a plain program's by a relative error of at most 0.00005.
Values sent between devices are 32-bit elements; how exact they have to be, the bound alone decides.
No kernel may reach another device: no remote copies, remote signals or barrier semaphores. Data moves between devices by JAX's collectives and lax.ppermute only.
A program may use at most 64 MiB of HBM per device.

v0:
```python
import functools

import jax
import jax.numpy as jnp
from jax import lax
from jax.experimental import pallas as pl
from jax.experimental.pallas import tpu as pltpu
from jax.sharding import PartitionSpec as P

LANES = 128
UNROLL = 16
BANKS = 2
PAD = 1
AXES = ("grp", "clu")
VMEM = pl.BlockSpec(memory_space=pltpu.VMEM)
SMEM = pl.BlockSpec(memory_space=pltpu.SMEM)
HBM = pl.BlockSpec(memory_space=pltpu.HBM)
DMA = pltpu.SemaphoreType.DMA


def in_hbm(*arrays):
    return tuple(pltpu.with_memory_space_constraint(a, pltpu.HBM) for a in arrays)


def in_vmem(*arrays):
    return tuple(pltpu.with_memory_space_constraint(a, pltpu.VMEM) for a in arrays)


def rows_for(quantities, groups):
    return -(-quantities // (LANES // groups))


def start_all(pairs, sems):
    copies = [pltpu.make_async_copy(src, dst, sems.at[i]) for i, (src, dst) in enumerate(pairs)]
    for copy in copies:
        copy.start()
    return copies


def pack_kernel(
    devices,
    pair_stride,
    groups,
    radiosity_hbm,
    area_hbm,
    cluster_group_hbm,
    source_device_hbm,
    source_slot_hbm,
    receiver_slot_hbm,
    ambient_hbm,
    out_ref,
    cluster_group_ref,
    source_device_ref,
    source_slot_ref,
    receiver_slot_ref,
    ambient_ref,
    radiosity_ref,
    area_ref,
    sems,
):
    channels, clusters, _ = radiosity_ref.shape
    per_row = LANES // groups
    copies = start_all(
        (
            (radiosity_hbm, radiosity_ref),
            (area_hbm, area_ref),
            (cluster_group_hbm, cluster_group_ref),
            (source_device_hbm, source_device_ref),
            (source_slot_hbm, source_slot_ref),
            (receiver_slot_hbm, receiver_slot_ref),
            (ambient_hbm, ambient_ref),
        ),
        sems,
    )
    for copy in copies[:3]:
        copy.wait()
    area = area_ref[...]
    sums = [
        jnp.sum(radiosity_ref[c] * area, axis=1, keepdims=True) for c in range(channels)
    ] + [jnp.sum(area, axis=1, keepdims=True)]
    lane = lax.broadcasted_iota(jnp.int32, (1, LANES), 1)
    info = [jnp.zeros((1, LANES), jnp.float32) for _ in range(rows_for(channels + 1, groups))]
    for q in range(channels + 1):
        for k in range(clusters):
            spot = (q % per_row) * groups + cluster_group_ref[k]
            info[q // per_row] += jnp.where(lane == spot, sums[q][k : k + 1], 0.0)
    half = clusters // 2
    halves = [
        [(0, k) for k in range(clusters)] + [(1, k) for k in range(half)],
        [(2, k) for k in range(clusters)] + [(1, k) for k in range(half, clusters)],
    ]
    block = len(halves[0]) + len(info)
    for d in range(devices):
        rows = [radiosity_ref[c, k : k + 1] for c, k in halves[d // pair_stride % 2]] + info
        for r, row in enumerate(rows):
            out_ref[d * block + r] = row
    for copy in copies[3:]:
        copy.wait()


def column_sums(acc, diagonal):
    column = jnp.sum(acc, axis=2, keepdims=True)
    spread = jnp.sum(jnp.where(diagonal, column, 0.0), axis=0)
    return jnp.sum(spread, axis=0, keepdims=True)


def diagonal_mask(width):
    shape = (width // 8, 8, width)
    patch = lax.broadcasted_iota(jnp.int32, shape, 0) * 8 + lax.broadcasted_iota(jnp.int32, shape, 1)
    return patch == lax.broadcasted_iota(jnp.int32, shape, 2)


def first_kernel(
    devices,
    groups,
    source_device_ref,
    source_slot_ref,
    receiver_slot_ref,
    cluster_group_ref,
    ambient_ref,
    own_ref,
    factors_ref,
    coupling_ref,
    rows_ref,
    *acc_refs,
):
    count, width, _ = factors_ref.shape
    clusters, blocks = acc_refs[0].shape[0], width // 8
    channels = ambient_ref.shape[0]
    half = clusters // 2
    block_rows = own_ref.shape[0] // devices
    own_rows = clusters + half
    per_row = LANES // groups

    for acc_ref in acc_refs:
        acc_ref[...] = jnp.zeros_like(acc_ref)

    def step(group, carried):
        for u in range(UNROLL):
            l = group * UNROLL + u
            k = receiver_slot_ref[l]
            place = source_device_ref[l] * block_rows + source_slot_ref[l]
            row = jnp.broadcast_to(own_ref[place], (8, width))
            acc_ref = acc_refs[u % len(acc_refs)]
            for b in range(blocks):
                acc_ref[k, b] += factors_ref[l, b * 8 : (b + 1) * 8, :] * row
        return carried

    lax.fori_loop(0, count // UNROLL, step, 0)

    totals = []
    for r in range(own_rows, block_rows):
        total = own_ref[r]
        for d in range(1, devices):
            total = total + own_ref[d * block_rows + r]
        totals.append(total)
    lane = lax.broadcasted_iota(jnp.int32, (1, LANES), 1)
    inside = lane < groups
    parts = []
    for q in range(channels + 1):
        row, shift = totals[q // per_row], (q % per_row) * groups
        part = pltpu.roll(row, LANES - shift, 1) if shift else row
        parts.append(jnp.where(inside, part, 0.0))
    group_area = jnp.where(inside, parts[channels], 1.0)
    all_area = jnp.sum(parts[channels], axis=1, keepdims=True)
    for c in range(channels):
        old_group = parts[c] / group_area
        root = ambient_ref[c] * (jnp.sum(parts[c], axis=1, keepdims=True) / all_area)
        for k in range(clusters):
            coupling = coupling_ref[pl.ds(cluster_group_ref[k], 1), :]
            coarse = (
                jnp.sum(coupling * old_group[:, :groups], axis=1, keepdims=True) / groups + root
            )
            rows_ref[clusters + c * clusters + k] = jnp.broadcast_to(coarse, (1, LANES))
    wide_area = group_area
    for q in range(1, per_row):
        wide_area = jnp.where(lane >= q * groups, pltpu.roll(group_area, q * groups, 1), wide_area)
    rows_ref[clusters + channels * clusters] = wide_area

    diagonal = diagonal_mask(width)
    for k in range(clusters):
        rows_ref[k] = column_sums(sum(acc_ref[k, :blocks] for acc_ref in acc_refs), diagonal)


def second_kernel(
    devices,
    groups,
    scale,
    source_device_ref,
    source_slot_ref,
    receiver_slot_ref,
    cluster_group_ref,
    own_ref,
    other_ref,
    factors_ref,
    rows_ref,
    emission_ref,
    reflectance_ref,
    area_ref,
    radiosity_ref,
    share_ref,
    *acc_refs,
):
    channels, clusters, width = emission_ref.shape
    count = factors_ref.shape[0]
    half = clusters // 2
    blocks = width // 8
    block_rows = own_ref.shape[0] // devices
    per_row = LANES // groups
    core = lax.rem(lax.axis_index("grp"), 2)

    for acc_ref in acc_refs:
        acc_ref[...] = jnp.zeros_like(acc_ref)

    def step(group, carried):
        for u in range(UNROLL):
            l = group * UNROLL + u
            k, slot = receiver_slot_ref[l], source_slot_ref[l]
            base = source_device_ref[l] * block_rows
            upper = (slot >= half).astype(jnp.int32)
            inner = base + slot - half * upper + clusters
            middle = jnp.where(
                upper == core,
                jnp.broadcast_to(own_ref[inner], (8, width)),
                jnp.broadcast_to(other_ref[inner], (8, width)),
            )
            rows = (middle, jnp.broadcast_to(other_ref[base + slot], (8, width)))
            acc_ref = acc_refs[u % len(acc_refs)]
            for b in range(blocks):
                f = factors_ref[l, b * 8 : (b + 1) * 8, :]
                for r in range(2):
                    acc_ref[k, r, b] += f * rows[r]
        return carried

    lax.fori_loop(0, count // UNROLL, step, 0)

    diagonal = diagonal_mask(width)
    lane = lax.broadcasted_iota(jnp.int32, (1, LANES), 1)
    shares = [jnp.zeros((1, LANES), jnp.float32) for _ in range(rows_for(channels, groups))]
    for k in range(clusters):
        mine = rows_ref[k]
        middle = column_sums(sum(acc_ref[k, 0, :blocks] for acc_ref in acc_refs), diagonal)
        others = column_sums(sum(acc_ref[k, 1, :blocks] for acc_ref in acc_refs), diagonal)
        by_channel = (
            jnp.where(core == 0, mine, others),
            middle,
            jnp.where(core == 0, others, mine),
        )
        for c in range(channels):
            coarse = rows_ref[clusters + c * clusters + k]
            new = emission_ref[c, k : k + 1] + reflectance_ref[c, k : k + 1] * (
                by_channel[c] * scale + coarse
            )
            radiosity_ref[c, k : k + 1] = new
            pulled = jnp.sum(new * area_ref[k : k + 1], axis=1, keepdims=True)
            spot = (c % per_row) * groups + cluster_group_ref[k]
            shares[c // per_row] += jnp.where(lane == spot, pulled, 0.0)
    for r in range(len(shares)):
        row = shares[r] / rows_ref[clusters + channels * clusters]
        for d in range(devices):
            share_ref[d * len(shares) + r] = row


def total_kernel(devices, groups, share_ref, new_ref, new_hbm, total_hbm, total_ref, sems):
    channels = new_ref.shape[0]
    per_row = LANES // groups
    count = share_ref.shape[0] // devices
    new_copy = pltpu.make_async_copy(new_ref, new_hbm, sems.at[0])
    new_copy.start()
    rows = []
    for r in range(count):
        total = share_ref[r]
        for d in range(1, devices):
            total = total + share_ref[d * count + r]
        rows.append(total)
    for c in range(channels):
        row, shift = rows[c // per_row], (c % per_row) * groups
        part = pltpu.roll(row, LANES - shift, 1) if shift else row
        total_ref[c : c + 1, :] = part[:, :groups]
    total_copy = pltpu.make_async_copy(total_ref, total_hbm, sems.at[1])
    total_copy.start()
    new_copy.wait()
    total_copy.wait()


def on_device(
    radiosity,
    form_factors,
    source_device,
    source_slot,
    receiver_slot,
    emission,
    reflectance,
    patch_area,
    cluster_group,
    group_coupling,
    ambient,
):
    clusters, channels, width = radiosity.shape
    count = form_factors.shape[0]
    groups = group_coupling.shape[0]
    devices = lax.axis_size("grp") * lax.axis_size("clu")
    scale = 2.0 * clusters / (width * count)
    pair_stride = lax.axis_size("clu")
    block = clusters + clusters // 2 + rows_for(channels + 1, groups)
    by_channel = functools.partial(jnp.transpose, axes=(1, 0, 2))
    f32, i32 = jnp.float32, jnp.int32
    own = pltpu.VMEM((channels, clusters, width), f32)

    packed, cluster_group, source_device, source_slot, receiver_slot, ambient = pl.pallas_call(
        functools.partial(pack_kernel, devices, pair_stride, groups),
        out_shape=(
            pltpu.VMEM((devices * block, 1, LANES), f32),
            pltpu.SMEM((clusters,), i32),
            pltpu.SMEM((count,), i32),
            pltpu.SMEM((count,), i32),
            pltpu.SMEM((count,), i32),
            pltpu.SMEM((channels,), f32),
        ),
        in_specs=[HBM] * 7,
        out_specs=(VMEM,) + (SMEM,) * 5,
        scratch_shapes=[
            pltpu.VMEM((channels, clusters, width), f32),
            pltpu.VMEM((clusters, width), f32),
            DMA((7,)),
        ],
        compiler_params=pltpu.CompilerParams(vmem_limit_bytes=4 << 20),
        cost_estimate=pl.CostEstimate(flops=10**10, transcendentals=0, bytes_accessed=10**8),
        name="pack",
    )(
        *in_hbm(
            by_channel(radiosity),
            patch_area,
            cluster_group,
            source_device[:, 0],
            source_slot,
            receiver_slot,
            ambient,
        )
    )
    own_half = lax.all_to_all(packed, AXES, split_axis=0, concat_axis=0, tiled=True)
    other_half = lax.ppermute(
        own_half, "grp", [(i, i ^ 1) for i in range(lax.axis_size("grp"))]
    )

    rows = pl.pallas_call(
        functools.partial(first_kernel, devices, groups),
        out_shape=pltpu.VMEM((clusters + channels * clusters + 1, 1, LANES), f32),
        in_specs=[SMEM] * 5 + [VMEM] * 3,
        out_specs=VMEM,
        scratch_shapes=[pltpu.VMEM((clusters, width // 8 + PAD, 8, width), f32)] * BANKS,
        compiler_params=pltpu.CompilerParams(vmem_limit_bytes=16 << 20),
        cost_estimate=pl.CostEstimate(flops=10**8, transcendentals=0, bytes_accessed=10**7),
        name="first",
    )(
        source_device,
        source_slot,
        receiver_slot,
        cluster_group,
        ambient,
        *in_vmem(own_half, form_factors, group_coupling),
    )
    share_rows = rows_for(channels, groups)
    new, share = pl.pallas_call(
        functools.partial(second_kernel, devices, groups, scale),
        out_shape=(own, pltpu.VMEM((devices * share_rows, 1, LANES), f32)),
        in_specs=[SMEM] * 4 + [VMEM] * 7,
        out_specs=(VMEM, VMEM),
        scratch_shapes=[pltpu.VMEM((clusters, 2, width // 8 + PAD, 8, width), f32)] * BANKS,
        compiler_params=pltpu.CompilerParams(vmem_limit_bytes=16 << 20),
        name="second",
    )(
        source_device,
        source_slot,
        receiver_slot,
        cluster_group,
        *in_vmem(
            own_half,
            other_half,
            form_factors,
            rows,
            by_channel(emission),
            by_channel(reflectance),
            patch_area,
        ),
    )
    shares = lax.all_to_all(share, AXES, split_axis=0, concat_axis=0, tiled=True)
    new, total = pl.pallas_call(
        functools.partial(total_kernel, devices, groups),
        out_shape=(
            pltpu.HBM((channels, clusters, width), f32),
            pltpu.HBM((channels, groups), f32),
        ),
        in_specs=[VMEM, VMEM],
        out_specs=(HBM, HBM),
        scratch_shapes=[pltpu.VMEM((channels, groups), f32), DMA((2,))],
        compiler_params=pltpu.CompilerParams(vmem_limit_bytes=4 << 20),
        name="total",
    )(*in_vmem(shares, new))
    return by_channel(new), total.T


def solution(mesh):
    split = AXES
    return jax.shard_map(
        on_device,
        mesh=mesh,
        in_specs=(
            P(split, None, None),
            P(split, None, None),
            P(split, None),
            P(split),
            P(split),
            P(split, None, None),
            P(split, None, None),
            P(split, None),
            P(split),
            P(),
            P(),
        ),
        out_specs=(P(split, None, None), P()),
        check_vma=False,
    )
```

profile of v0, /device:TPU:0, one launch (start us, length us, event | category | flops | bytes accessed | tf_op | source)
XLA Modules:
  0.0 29.8 jit_solution(17330443178148075647)
XLA Ops:
  0.6 0.0 copy-start
  0.6 0.0 copy-start.1
  0.7 1.1 %pack.1 = (f32[224,1,128]{2,1,0:T(1,128)S(1)}, s32[4]{0:T(128)S(4)}, s32[128]{0:T(128)S(4)}, s32[128]{0:T(128)S(4)}, s32[128]{0:T(128)S(4)}, /*index=5*/f32[3]{0:T(128)S(4)}) custom-call(f32[3,4,128]{2,1,0:T(4,128)} %bitcast.8, f32[4,128]{1,0:T(4,128)} %area_ref.1, s32[4]{0:T(128)} %cluster_group_hbm.1, s32[128]{0:T(128)} %bitcast.11, s32[128]{0:T(128)} %source_slot_hbm.1, ...), custom_call_target="tpu_custom_call" | custom-call | flops 10000000000 | bytes 100000000 | tf_op jit(solution)/shard_map/pack/pallas_call | solution.py:310
  1.7 0.0 copy-start.2
  1.7 0.0 copy-start.3
  1.7 0.0 copy-start.4
  1.8 14.8 %all_to_all.10.own_ref = f32[224,1,128]{2,1,0:T(1,128)S(1)} all-to-all(f32[224,1,128]{2,1,0:T(1,128)S(1)} %get-tuple-element.16), channel_id=1, replica_groups=mesh['grp'=4,'clu'=8] {'grp','clu'}, dimensions={0} | all-to-all | bytes 229376 | tf_op jit(solution)/shard_map/all_to_all | solution.py:341
  16.6 0.1 collective-permute-start
  16.7 0.0 copy-done
  16.7 0.0 copy-done.1
  16.7 1.3 %first.1.rows_ref = f32[17,1,128]{2,1,0:T(1,128)S(1)} custom-call(s32[128]{0:T(128)S(4)} %get-tuple-element.12.source_device_ref, s32[128]{0:T(128)S(4)} %get-tuple-element.13.source_slot_ref, s32[128]{0:T(128)S(4)} %get-tuple-element.14.receiver_slot_ref, s32[4]{0:T(128)S(4)} %get-tuple-element.15.cluster_group_ref, f32[3]{0:T(128)S(4)} %get-tuple-element.17.ambient_ref, ...), custom_call_target="tpu_custom_call" | custom-call | flops 100000000 | bytes 10000000 | tf_op jit(solution)/shard_map/first/pallas_call | solution.py:346
  18.1 0.0 collective-permute-done.other_ref
  18.1 0.0 copy-done.2
  18.1 0.0 copy-done.3
  18.1 0.0 copy-done.4
  18.1 2.0 %second.1 = (f32[3,4,128]{2,1,0:T(4,128)S(1)}, f32[32,1,128]{2,1,0:T(1,128)S(1)}) custom-call(s32[128]{0:T(128)S(4)} %get-tuple-element.12.source_device_ref, s32[128]{0:T(128)S(4)} %get-tuple-element.13.source_slot_ref, s32[128]{0:T(128)S(4)} %get-tuple-element.14.receiver_slot_ref, s32[4]{0:T(128)S(4)} %get-tuple-element.15.cluster_group_ref, ...), custom_call_target="tpu_custom_call" | custom-call | tf_op jit(solution)/shard_map/second/pallas_call | solution.py:364
  20.1 9.0 %all_to_all.11.share_ref = f32[32,1,128]{2,1,0:T(1,128)S(1)} all-to-all(f32[32,1,128]{2,1,0:T(1,128)S(1)} %get-tuple-element.18), channel_id=1, replica_groups=mesh['grp'=4,'clu'=8] {'grp','clu'}, dimensions={0} | all-to-all | bytes 32768 | tf_op jit(solution)/shard_map/all_to_all | solution.py:387
  29.2 0.7 %total.1 = (f32[3,4,128]{2,1,0:T(4,128)}, f32[3,16]{1,0:T(4,128)}) custom-call(f32[32,1,128]{2,1,0:T(1,128)S(1)} %all_to_all.11.share_ref, f32[3,4,128]{2,1,0:T(4,128)S(1)} %get-tuple-element.19.new_ref), custom_call_target="tpu_custom_call" | custom-call | tf_op jit(solution)/shard_map/total/pallas_call | solution.py:388
Async XLA Ops:
  0.6 16.1 %copy-start = (f32[128,128,128]{2,1,0:T(8,128)S(1)}, f32[128,128,128]{2,1,0:T(8,128)}, u32[]{:S(2)}) copy-start(f32[128,128,128]{2,1,0:T(8,128)} %factors_ref.3) | copy-start | bytes 25165828
  0.6 16.1 %copy-start.1 = (f32[16,16]{1,0:T(8,128)S(1)}, f32[16,16]{1,0:T(8,128)}, u32[]{:S(2)}) copy-start(f32[16,16]{1,0:T(8,128)} %coupling_ref.1) | copy-start | bytes 3076
  1.7 16.4 %copy-start.2 = (f32[4,3,128]{2,0,1:T(4,128)S(1)}, f32[4,3,128]{2,0,1:T(4,128)}, u32[]{:S(2)}) copy-start(f32[4,3,128]{2,0,1:T(4,128)} %param.16) | copy-start | bytes 18436
  1.7 16.4 %copy-start.3 = (f32[4,3,128]{2,0,1:T(4,128)S(1)}, f32[4,3,128]{2,0,1:T(4,128)}, u32[]{:S(2)}) copy-start(f32[4,3,128]{2,0,1:T(4,128)} %param.17) | copy-start | bytes 18436
  1.7 16.4 %copy-start.4 = (f32[4,128]{1,0:T(4,128)S(1)}, f32[4,128]{1,0:T(4,128)}, u32[]{:S(2)}) copy-start(f32[4,128]{1,0:T(4,128)} %area_ref.1) | copy-start | bytes 6148
  16.6 1.5 %collective-permute-start = (f32[224,1,128]{2,1,0:T(1,128)S(1)}, f32[224,1,128]{2,1,0:T(1,128)S(1)}, u32[]{:S(2)}, u32[]{:S(2)}) collective-permute-start(f32[224,1,128]{2,1,0:T(1,128)S(1)} %all_to_all.10.own_ref), channel_id=1, source_target_pairs={{0,8},{8,0},{16,24},{24,16},{1,9},{9,1},{17,25},{25,17},{2,10},{10... | collective-permute-start | bytes 344072 | tf_op jit(solution)/shard_map/ppermute | solution.py:342
where the time goes:
time: 30 us; the launch traced here: 29.8 us
  blocking collectives  23.9 us (80%)
  Pallas kernels  5.09 us (17%)
  between operations  0.73 us (2%)
    all_to_all x1, blocking collectives, on_device(): lax.all_to_all(packed, AXES, split_axis=0, concat_axis=0, tiled=True)  14.8 us
    all_to_all x1, blocking collectives, on_device(): lax.all_to_all(share, AXES, split_axis=0, concat_axis=0, tiled=True)  9.03 us
    pallas_call x1, Pallas kernels, on_device(): pl.pallas_call(functools.partial(second_kernel, devices, groups, scale),...  2 us
    pallas_call x1, Pallas kernels, on_device(): pl.pallas_call(functools.partial(first_kernel, devices, groups), out_shap...  1.35 us
    pallas_call x1, Pallas kernels, on_device(): pl.pallas_call(functools.partial(pack_kernel, devices, pair_stride, group...  1.06 us
    pallas_call x1, Pallas kernels, on_device(): pl.pallas_call(functools.partial(total_kernel, devices, groups), out_shap...  0.68 us
  transfers between devices with their start and end apart: 1, of which 0 were waited for; matrix products, arithmetic and copies ran while one was open for 0% of the time, Pallas kernels for 5%

commit v1 on v0

--- a/solution.py
+++ b/solution.py
@@ -28,6 +28,29 @@
 
 def rows_for(quantities, groups):
     return -(-quantities // (LANES // groups))
+
+
+def place(sums, cluster_group_ref, groups):
+    clusters = sums[0].shape[0]
+    per_row = LANES // groups
+    lane = lax.broadcasted_iota(jnp.int32, (clusters, LANES), 1)
+    cluster = lax.broadcasted_iota(jnp.int32, (clusters, LANES), 0)
+    group = jnp.full((clusters, LANES), cluster_group_ref[0], jnp.int32)
+    for k in range(1, clusters):
+        group = jnp.where(cluster == k, cluster_group_ref[k], group)
+    rows = []
+    for first in range(0, len(sums), per_row):
+        spread = jnp.zeros((clusters, LANES), jnp.float32)
+        for q in range(first, min(first + per_row, len(sums))):
+            spread = jnp.where(lane == (q - first) * groups + group, sums[q], spread)
+        rows.append(jnp.sum(spread, axis=0, keepdims=True))
+    return rows
+
+
+def tree_sum(values):
+    while len(values) > 1:
+        values = [sum(values[i : i + 2]) for i in range(0, len(values), 2)]
+    return values[0]
 
 
 def start_all(pairs, sems):
@@ -78,12 +101,7 @@
     sums = [
         jnp.sum(radiosity_ref[c] * area, axis=1, keepdims=True) for c in range(channels)
     ] + [jnp.sum(area, axis=1, keepdims=True)]
-    lane = lax.broadcasted_iota(jnp.int32, (1, LANES), 1)
-    info = [jnp.zeros((1, LANES), jnp.float32) for _ in range(rows_for(channels + 1, groups))]
-    for q in range(channels + 1):
-        for k in range(clusters):
-            spot = (q % per_row) * groups + cluster_group_ref[k]
-            info[q // per_row] += jnp.where(lane == spot, sums[q][k : k + 1], 0.0)
+    info = place(sums, cluster_group_ref, groups)
     half = clusters // 2
     halves = [
         [(0, k) for k in range(clusters)] + [(1, k) for k in range(half)],
@@ -146,14 +164,10 @@
                 acc_ref[k, b] += factors_ref[l, b * 8 : (b + 1) * 8, :] * row
         return carried
 
-    lax.fori_loop(0, count // UNROLL, step, 0)
-
-    totals = []
-    for r in range(own_rows, block_rows):
-        total = own_ref[r]
-        for d in range(1, devices):
-            total = total + own_ref[d * block_rows + r]
-        totals.append(total)
+    totals = [
+        tree_sum([own_ref[d * block_rows + r] for d in range(devices)])
+        for r in range(own_rows, block_rows)
+    ]
     lane = lax.broadcasted_iota(jnp.int32, (1, LANES), 1)
     inside = lane < groups
     parts = []
@@ -175,7 +189,10 @@
     wide_area = group_area
     for q in range(1, per_row):
         wide_area = jnp.where(lane >= q * groups, pltpu.roll(group_area, q * groups, 1), wide_area)
-    rows_ref[clusters + channels * clusters] = wide_area
+    rows_ref[clusters + channels * clusters] = 1.0 / wide_area
+
+    step(0, 0)
+    lax.fori_loop(1, count // UNROLL, step, 0)
 
     diagonal = diagonal_mask(width)
     for k in range(clusters):
@@ -235,8 +252,6 @@
     lax.fori_loop(0, count // UNROLL, step, 0)
 
     diagonal = diagonal_mask(width)
-    lane = lax.broadcasted_iota(jnp.int32, (1, LANES), 1)
-    shares = [jnp.zeros((1, LANES), jnp.float32) for _ in range(rows_for(channels, groups))]
     for k in range(clusters):
         mine = rows_ref[k]
         middle = column_sums(sum(acc_ref[k, 0, :blocks] for acc_ref in acc_refs), diagonal)
@@ -248,15 +263,15 @@
         )
         for c in range(channels):
             coarse = rows_ref[clusters + c * clusters + k]
-            new = emission_ref[c, k : k + 1] + reflectance_ref[c, k : k + 1] * (
-                by_channel[c] * scale + coarse
-            )
-            radiosity_ref[c, k : k + 1] = new
-            pulled = jnp.sum(new * area_ref[k : k + 1], axis=1, keepdims=True)
-            spot = (c % per_row) * groups + cluster_group_ref[k]
-            shares[c // per_row] += jnp.where(lane == spot, pulled, 0.0)
+            radiosity_ref[c, k : k + 1] = emission_ref[c, k : k + 1] + reflectance_ref[
+                c, k : k + 1
+            ] * (by_channel[c] * scale + coarse)
+    pulled = [
+        jnp.sum(radiosity_ref[c] * area_ref[...], axis=1, keepdims=True) for c in range(channels)
+    ]
+    shares = place(pulled, cluster_group_ref, groups)
     for r in range(len(shares)):
-        row = shares[r] / rows_ref[clusters + channels * clusters]
+        row = shares[r] * rows_ref[clusters + channels * clusters]
         for d in range(devices):
             share_ref[d * len(shares) + r] = row
 
@@ -267,12 +282,7 @@
     count = share_ref.shape[0] // devices
     new_copy = pltpu.make_async_copy(new_ref, new_hbm, sems.at[0])
     new_copy.start()
-    rows = []
-    for r in range(count):
-        total = share_ref[r]
-        for d in range(1, devices):
-            total = total + share_ref[d * count + r]
-        rows.append(total)
+    rows = [tree_sum([share_ref[d * count + r] for d in range(devices)]) for r in range(count)]
     for c in range(channels):
         row, shift = rows[c // per_row], (c % per_row) * groups
         part = pltpu.roll(row, LANES - shift, 1) if shift else row

time: 30 us -> 30 us (level)
  transfers between devices with their start and end apart: 1 -> 1, of which waited for: 0 -> 0; matrix products, arithmetic and copies ran while one was open for 0% -> 0% of each run, Pallas kernels for 5% -> 4%
where the time goes in v1:
time: 30 us; the launch traced here: 29.8 us
  blocking collectives  23.9 us (80%)
  Pallas kernels  5.03 us (17%)
  between operations  0.73 us (2%)
    all_to_all x1, blocking collectives, on_device(): lax.all_to_all(packed, AXES, split_axis=0, concat_axis=0, tiled=True)  14.8 us
    all_to_all x1, blocking collectives, on_device(): lax.all_to_all(share, AXES, split_axis=0, concat_axis=0, tiled=True)  9.04 us
    pallas_call x1, Pallas kernels, on_device(): pl.pallas_call(functools.partial(second_kernel, devices, groups, scale),...  1.99 us
    pallas_call x1, Pallas kernels, on_device(): pl.pallas_call(functools.partial(first_kernel, devices, groups), out_shap...  1.32 us
    pallas_call x1, Pallas kernels, on_device(): pl.pallas_call(functools.partial(pack_kernel, devices, pair_stride, group...  1.05 us
    pallas_call x1, Pallas kernels, on_device(): pl.pallas_call(functools.partial(total_kernel, devices, groups), out_shap...  0.66 us
  transfers between devices with their start and end apart: 1, of which 0 were waited for; matrix products, arithmetic and copies ran while one was open for 0% of the time, Pallas kernels for 4%

profile of v1, /device:TPU:0, one launch (start us, length us, event | category | flops | bytes accessed | tf_op | source)
XLA Modules:
  0.0 29.8 jit_solution(9554445056378633623)
XLA Ops:
  0.6 0.0 copy-start
  0.6 0.0 copy-start.1
  0.7 1.1 %pack.1 = (f32[224,1,128]{2,1,0:T(1,128)S(1)}, s32[4]{0:T(128)S(4)}, s32[128]{0:T(128)S(4)}, s32[128]{0:T(128)S(4)}, s32[128]{0:T(128)S(4)}, /*index=5*/f32[3]{0:T(128)S(4)}) custom-call(f32[3,4,128]{2,1,0:T(4,128)} %bitcast.8, f32[4,128]{1,0:T(4,128)} %area_ref.1, s32[4]{0:T(128)} %cluster_group_hbm.1, s32[128]{0:T(128)} %bitcast.11, s32[128]{0:T(128)} %source_slot_hbm.1, ...), custom_call_target="tpu_custom_call" | custom-call | flops 10000000000 | bytes 100000000 | tf_op jit(solution)/shard_map/pack/pallas_call | solution.py:320
  1.7 0.0 copy-start.2
  1.7 0.0 copy-start.3
  1.7 0.0 copy-start.4
  1.7 14.8 %all_to_all.10.own_ref = f32[224,1,128]{2,1,0:T(1,128)S(1)} all-to-all(f32[224,1,128]{2,1,0:T(1,128)S(1)} %get-tuple-element.16), channel_id=1, replica_groups=mesh['grp'=4,'clu'=8] {'grp','clu'}, dimensions={0} | all-to-all | bytes 229376 | tf_op jit(solution)/shard_map/all_to_all | solution.py:351
  16.6 0.1 collective-permute-start
  16.7 0.0 copy-done
  16.7 0.0 copy-done.1
  16.7 1.3 %first.1.rows_ref = f32[17,1,128]{2,1,0:T(1,128)S(1)} custom-call(s32[128]{0:T(128)S(4)} %get-tuple-element.12.source_device_ref, s32[128]{0:T(128)S(4)} %get-tuple-element.13.source_slot_ref, s32[128]{0:T(128)S(4)} %get-tuple-element.14.receiver_slot_ref, s32[4]{0:T(128)S(4)} %get-tuple-element.15.cluster_group_ref, f32[3]{0:T(128)S(4)} %get-tuple-element.17.ambient_ref, ...), custom_call_target="tpu_custom_call" | custom-call | flops 100000000 | bytes 10000000 | tf_op jit(solution)/shard_map/first/pallas_call | solution.py:356
  18.0 0.0 collective-permute-done.other_ref
  18.1 0.0 copy-done.2
  18.1 0.0 copy-done.3
  18.1 0.0 copy-done.4
  18.1 2.0 %second.1 = (f32[3,4,128]{2,1,0:T(4,128)S(1)}, f32[32,1,128]{2,1,0:T(1,128)S(1)}) custom-call(s32[128]{0:T(128)S(4)} %get-tuple-element.12.source_device_ref, s32[128]{0:T(128)S(4)} %get-tuple-element.13.source_slot_ref, s32[128]{0:T(128)S(4)} %get-tuple-element.14.receiver_slot_ref, s32[4]{0:T(128)S(4)} %get-tuple-element.15.cluster_group_ref, ...), custom_call_target="tpu_custom_call" | custom-call | tf_op jit(solution)/shard_map/second/pallas_call | solution.py:374
  20.1 9.0 %all_to_all.11.share_ref = f32[32,1,128]{2,1,0:T(1,128)S(1)} all-to-all(f32[32,1,128]{2,1,0:T(1,128)S(1)} %get-tuple-element.18), channel_id=1, replica_groups=mesh['grp'=4,'clu'=8] {'grp','clu'}, dimensions={0} | all-to-all | bytes 32768 | tf_op jit(solution)/shard_map/all_to_all | solution.py:397
  29.1 0.7 %total.1 = (f32[3,4,128]{2,1,0:T(4,128)}, f32[3,16]{1,0:T(4,128)}) custom-call(f32[32,1,128]{2,1,0:T(1,128)S(1)} %all_to_all.11.share_ref, f32[3,4,128]{2,1,0:T(4,128)S(1)} %get-tuple-element.19.new_ref), custom_call_target="tpu_custom_call" | custom-call | tf_op jit(solution)/shard_map/total/pallas_call | solution.py:398
Async XLA Ops:
  0.6 16.1 %copy-start = (f32[128,128,128]{2,1,0:T(8,128)S(1)}, f32[128,128,128]{2,1,0:T(8,128)}, u32[]{:S(2)}) copy-start(f32[128,128,128]{2,1,0:T(8,128)} %factors_ref.3) | copy-start | bytes 25165828
  0.6 16.1 %copy-start.1 = (f32[16,16]{1,0:T(8,128)S(1)}, f32[16,16]{1,0:T(8,128)}, u32[]{:S(2)}) copy-start(f32[16,16]{1,0:T(8,128)} %coupling_ref.1) | copy-start | bytes 3076
  1.7 16.3 %copy-start.2 = (f32[4,3,128]{2,0,1:T(4,128)S(1)}, f32[4,3,128]{2,0,1:T(4,128)}, u32[]{:S(2)}) copy-start(f32[4,3,128]{2,0,1:T(4,128)} %param.16) | copy-start | bytes 18436
  1.7 16.3 %copy-start.3 = (f32[4,3,128]{2,0,1:T(4,128)S(1)}, f32[4,3,128]{2,0,1:T(4,128)}, u32[]{:S(2)}) copy-start(f32[4,3,128]{2,0,1:T(4,128)} %param.17) | copy-start | bytes 18436
  1.7 16.3 %copy-start.4 = (f32[4,128]{1,0:T(4,128)S(1)}, f32[4,128]{1,0:T(4,128)}, u32[]{:S(2)}) copy-start(f32[4,128]{1,0:T(4,128)} %area_ref.1) | copy-start | bytes 6148
  16.6 1.5 %collective-permute-start = (f32[224,1,128]{2,1,0:T(1,128)S(1)}, f32[224,1,128]{2,1,0:T(1,128)S(1)}, u32[]{:S(2)}, u32[]{:S(2)}) collective-permute-start(f32[224,1,128]{2,1,0:T(1,128)S(1)} %all_to_all.10.own_ref), channel_id=1, source_target_pairs={{0,8},{8,0},{16,24},{24,16},{1,9},{9,1},{17,25},{25,17},{2,10},{10... | collective-permute-start | bytes 344072 | tf_op jit(solution)/shard_map/ppermute | solution.py:352

commit v2 on v1

--- a/solution.py
+++ b/solution.py
@@ -73,9 +73,7 @@
     ambient_hbm,
     out_ref,
     cluster_group_ref,
-    source_device_ref,
-    source_slot_ref,
-    receiver_slot_ref,
+    index_ref,
     ambient_ref,
     radiosity_ref,
     area_ref,
@@ -88,13 +86,13 @@
             (radiosity_hbm, radiosity_ref),
             (area_hbm, area_ref),
             (cluster_group_hbm, cluster_group_ref),
-            (source_device_hbm, source_device_ref),
-            (source_slot_hbm, source_slot_ref),
-            (receiver_slot_hbm, receiver_slot_ref),
             (ambient_hbm, ambient_ref),
         ),
         sems,
     )
+    count = source_slot_hbm.shape[0]
+    for i, array in enumerate((source_device_hbm, source_slot_hbm, receiver_slot_hbm)):
+        pltpu.make_async_copy(array, index_ref.at[pl.ds(i * count, count)], sems.at[4]).start()
     for copy in copies[:3]:
         copy.wait()
     area = area_ref[...]
@@ -112,8 +110,8 @@
         rows = [radiosity_ref[c, k : k + 1] for c, k in halves[d // pair_stride % 2]] + info
         for r, row in enumerate(rows):
             out_ref[d * block + r] = row
-    for copy in copies[3:]:
-        copy.wait()
+    copies[3].wait()
+    pltpu.make_async_copy(index_ref, index_ref, sems.at[4]).wait()
 
 
 def column_sums(acc, diagonal):
@@ -131,9 +129,7 @@
 def first_kernel(
     devices,
     groups,
-    source_device_ref,
-    source_slot_ref,
-    receiver_slot_ref,
+    index_ref,
     cluster_group_ref,
     ambient_ref,
     own_ref,
@@ -156,8 +152,8 @@
     def step(group, carried):
         for u in range(UNROLL):
             l = group * UNROLL + u
-            k = receiver_slot_ref[l]
-            place = source_device_ref[l] * block_rows + source_slot_ref[l]
+            k = index_ref[2 * count + l]
+            place = index_ref[l] * block_rows + index_ref[count + l]
             row = jnp.broadcast_to(own_ref[place], (8, width))
             acc_ref = acc_refs[u % len(acc_refs)]
             for b in range(blocks):
@@ -203,9 +199,7 @@
     devices,
     groups,
     scale,
-    source_device_ref,
-    source_slot_ref,
-    receiver_slot_ref,
+    index_ref,
     cluster_group_ref,
     own_ref,
     other_ref,
@@ -232,8 +226,8 @@
     def step(group, carried):
         for u in range(UNROLL):
             l = group * UNROLL + u
-            k, slot = receiver_slot_ref[l], source_slot_ref[l]
-            base = source_device_ref[l] * block_rows
+            k, slot = index_ref[2 * count + l], index_ref[count + l]
+            base = index_ref[l] * block_rows
             upper = (slot >= half).astype(jnp.int32)
             inner = base + slot - half * upper + clusters
             middle = jnp.where(
@@ -317,22 +311,20 @@
     f32, i32 = jnp.float32, jnp.int32
     own = pltpu.VMEM((channels, clusters, width), f32)
 
-    packed, cluster_group, source_device, source_slot, receiver_slot, ambient = pl.pallas_call(
+    packed, cluster_group, index, ambient = pl.pallas_call(
         functools.partial(pack_kernel, devices, pair_stride, groups),
         out_shape=(
             pltpu.VMEM((devices * block, 1, LANES), f32),
             pltpu.SMEM((clusters,), i32),
-            pltpu.SMEM((count,), i32),
-            pltpu.SMEM((count,), i32),
-            pltpu.SMEM((count,), i32),
+            pltpu.SMEM((3 * count,), i32),
             pltpu.SMEM((channels,), f32),
         ),
         in_specs=[HBM] * 7,
-        out_specs=(VMEM,) + (SMEM,) * 5,
+        out_specs=(VMEM,) + (SMEM,) * 3,
         scratch_shapes=[
             pltpu.VMEM((channels, clusters, width), f32),
             pltpu.VMEM((clusters, width), f32),
-            DMA((7,)),
+            DMA((5,)),
         ],
         compiler_params=pltpu.CompilerParams(vmem_limit_bytes=4 << 20),
         cost_estimate=pl.CostEstimate(flops=10**10, transcendentals=0, bytes_accessed=10**8),
@@ -356,16 +348,14 @@
     rows = pl.pallas_call(
         functools.partial(first_kernel, devices, groups),
         out_shape=pltpu.VMEM((clusters + channels * clusters + 1, 1, LANES), f32),
-        in_specs=[SMEM] * 5 + [VMEM] * 3,
+        in_specs=[SMEM] * 3 + [VMEM] * 3,
         out_specs=VMEM,
-        scratch_shapes=[pltpu.VMEM((clusters, width // 8 + PAD, 8, width), f32)] * BANKS,
+        scratch_shapes=[pltpu.VMEM((clusters, width // 8 + 2 * PAD, 8, width), f32)] * BANKS,
         compiler_params=pltpu.CompilerParams(vmem_limit_bytes=16 << 20),
         cost_estimate=pl.CostEstimate(flops=10**8, transcendentals=0, bytes_accessed=10**7),
         name="first",
     )(
-        source_device,
-        source_slot,
-        receiver_slot,
+        index,
         cluster_group,
         ambient,
         *in_vmem(own_half, form_factors, group_coupling),
@@ -374,15 +364,13 @@
     new, share = pl.pallas_call(
         functools.partial(second_kernel, devices, groups, scale),
         out_shape=(own, pltpu.VMEM((devices * share_rows, 1, LANES), f32)),
-        in_specs=[SMEM] * 4 + [VMEM] * 7,
+        in_specs=[SMEM] * 2 + [VMEM] * 7,
         out_specs=(VMEM, VMEM),
         scratch_shapes=[pltpu.VMEM((clusters, 2, width // 8 + PAD, 8, width), f32)] * BANKS,
         compiler_params=pltpu.CompilerParams(vmem_limit_bytes=16 << 20),
         name="second",
     )(
-        source_device,
-        source_slot,
-        receiver_slot,
+        index,
         cluster_group,
         *in_vmem(
             own_half,

time: 30 us -> 29.9 us (level)
  no operation moved by 1% of the time
where the time goes in v2:
time: 29.9 us; the launch traced here: 29.7 us
  blocking collectives  23.9 us (80%)
  Pallas kernels  4.99 us (17%)
  between operations  0.73 us (2%)
    all_to_all x1, blocking collectives, on_device(): lax.all_to_all(packed, AXES, split_axis=0, concat_axis=0, tiled=True)  14.8 us
    all_to_all x1, blocking collectives, on_device(): lax.all_to_all(share, AXES, split_axis=0, concat_axis=0, tiled=True)  9.03 us
    pallas_call x1, Pallas kernels, on_device(): pl.pallas_call(functools.partial(second_kernel, devices, groups, scale),...  2.01 us
    pallas_call x1, Pallas kernels, on_device(): pl.pallas_call(functools.partial(first_kernel, devices, groups), out_shap...  1.3 us
    pallas_call x1, Pallas kernels, on_device(): pl.pallas_call(functools.partial(pack_kernel, devices, pair_stride, group...  1.01 us
    pallas_call x1, Pallas kernels, on_device(): pl.pallas_call(functools.partial(total_kernel, devices, groups), out_shap...  0.66 us
  transfers between devices with their start and end apart: 1, of which 0 were waited for; matrix products, arithmetic and copies ran while one was open for 0% of the time, Pallas kernels for 4%

profile of v2, /device:TPU:0, one launch (start us, length us, event | category | flops | bytes accessed | tf_op | source)
XLA Modules:
  0.0 29.7 jit_solution(16852720240718880493)
XLA Ops:
  0.6 0.0 copy-start
  0.6 0.0 copy-start.1
  0.7 1.0 %pack.1 = (f32[224,1,128]{2,1,0:T(1,128)S(1)}, s32[4]{0:T(128)S(4)}, s32[384]{0:T(512)S(4)}, f32[3]{0:T(128)S(4)}) custom-call(f32[3,4,128]{2,1,0:T(4,128)} %bitcast.8, f32[4,128]{1,0:T(4,128)} %area_ref.1, s32[4]{0:T(128)} %cluster_group_hbm.1, s32[128]{0:T(128)} %bitcast.11, s32[128]{0:T(128)} %source_slot_hbm.1, s32[128]{0:T(128)} %receiver_slot_hbm.1, ...), custom_call_target="tpu_custom_call" | custom-call | flops 10000000000 | bytes 100000000 | tf_op jit(solution)/shard_map/pack/pallas_call | solution.py:314
  1.7 0.0 copy-start.2
  1.7 0.0 copy-start.3
  1.7 0.0 copy-start.4
  1.7 14.8 %all_to_all.10.own_ref = f32[224,1,128]{2,1,0:T(1,128)S(1)} all-to-all(f32[224,1,128]{2,1,0:T(1,128)S(1)} %get-tuple-element.12), channel_id=1, replica_groups=mesh['grp'=4,'clu'=8] {'grp','clu'}, dimensions={0} | all-to-all | bytes 229376 | tf_op jit(solution)/shard_map/all_to_all | solution.py:343
  16.6 0.1 collective-permute-start
  16.7 0.0 copy-done
  16.7 0.0 copy-done.1
  16.7 1.3 %first.1.rows_ref = f32[17,1,128]{2,1,0:T(1,128)S(1)} custom-call(s32[384]{0:T(512)S(4)} %get-tuple-element.10.index_ref, s32[4]{0:T(128)S(4)} %get-tuple-element.11.cluster_group_ref, f32[3]{0:T(128)S(4)} %get-tuple-element.13.ambient_ref, f32[224,1,128]{2,1,0:T(1,128)S(1)} %all_to_all.10.own_ref, f32[128,128,128]{2,1,0:T(8,128)S(1)} %copy-done, ...), custom_call_target="tpu_custom_call" | custom-call | flops 100000000 | bytes 10000000 | tf_op jit(solution)/shard_map/first/pallas_call | solution.py:348
  18.0 0.0 collective-permute-done.other_ref
  18.0 0.0 copy-done.2
  18.0 0.0 copy-done.3
  18.0 0.0 copy-done.4
  18.0 2.0 %second.1 = (f32[3,4,128]{2,1,0:T(4,128)S(1)}, f32[32,1,128]{2,1,0:T(1,128)S(1)}) custom-call(s32[384]{0:T(512)S(4)} %get-tuple-element.10.index_ref, s32[4]{0:T(128)S(4)} %get-tuple-element.11.cluster_group_ref, f32[224,1,128]{2,1,0:T(1,128)S(1)} %all_to_all.10.own_ref, f32[224,1,128]{2,1,0:T(1,128)S(1)} %collective-permute-done.other_ref, ...), custom_call_target="tpu_custom_call" | custom-call | tf_op jit(solution)/shard_map/second/pallas_call | solution.py:364
  20.0 9.0 %all_to_all.11.share_ref = f32[32,1,128]{2,1,0:T(1,128)S(1)} all-to-all(f32[32,1,128]{2,1,0:T(1,128)S(1)} %get-tuple-element.14), channel_id=1, replica_groups=mesh['grp'=4,'clu'=8] {'grp','clu'}, dimensions={0} | all-to-all | bytes 32768 | tf_op jit(solution)/shard_map/all_to_all | solution.py:385
  29.1 0.7 %total.1 = (f32[3,4,128]{2,1,0:T(4,128)}, f32[3,16]{1,0:T(4,128)}) custom-call(f32[32,1,128]{2,1,0:T(1,128)S(1)} %all_to_all.11.share_ref, f32[3,4,128]{2,1,0:T(4,128)S(1)} %get-tuple-element.15.new_ref), custom_call_target="tpu_custom_call" | custom-call | tf_op jit(solution)/shard_map/total/pallas_call | solution.py:386
Async XLA Ops:
  0.6 16.0 %copy-start = (f32[128,128,128]{2,1,0:T(8,128)S(1)}, f32[128,128,128]{2,1,0:T(8,128)}, u32[]{:S(2)}) copy-start(f32[128,128,128]{2,1,0:T(8,128)} %factors_ref.3) | copy-start | bytes 25165828
  0.6 16.0 %copy-start.1 = (f32[16,16]{1,0:T(8,128)S(1)}, f32[16,16]{1,0:T(8,128)}, u32[]{:S(2)}) copy-start(f32[16,16]{1,0:T(8,128)} %coupling_ref.1) | copy-start | bytes 3076
  1.7 16.3 %copy-start.2 = (f32[4,3,128]{2,0,1:T(4,128)S(1)}, f32[4,3,128]{2,0,1:T(4,128)}, u32[]{:S(2)}) copy-start(f32[4,3,128]{2,0,1:T(4,128)} %param.16) | copy-start | bytes 18436
  1.7 16.3 %copy-start.3 = (f32[4,3,128]{2,0,1:T(4,128)S(1)}, f32[4,3,128]{2,0,1:T(4,128)}, u32[]{:S(2)}) copy-start(f32[4,3,128]{2,0,1:T(4,128)} %param.17) | copy-start | bytes 18436
  1.7 16.3 %copy-start.4 = (f32[4,128]{1,0:T(4,128)S(1)}, f32[4,128]{1,0:T(4,128)}, u32[]{:S(2)}) copy-start(f32[4,128]{1,0:T(4,128)} %area_ref.1) | copy-start | bytes 6148
  16.6 1.4 %collective-permute-start = (f32[224,1,128]{2,1,0:T(1,128)S(1)}, f32[224,1,128]{2,1,0:T(1,128)S(1)}, u32[]{:S(2)}, u32[]{:S(2)}) collective-permute-start(f32[224,1,128]{2,1,0:T(1,128)S(1)} %all_to_all.10.own_ref), channel_id=1, source_target_pairs={{0,8},{8,0},{16,24},{24,16},{1,9},{9,1},{17,25},{25,17},{2,10},{10... | collective-permute-start | bytes 344072 | tf_op jit(solution)/shard_map/ppermute | solution.py:344
